TPU v7x, 512 devices: a whole 4x8x8 slice. The times are simulated.
512 devices in a mesh: blk: 128 (over z_lo, y, x), freq: 4 (over z_hi, core).
Axes of the slice: x: 4, y: 8, z: 8 (z_hi: 2, z_lo: 4; z = z_hi * 4 + z_lo), core: 2. Of those that a mesh axis runs over, the one named last changes fastest.
Arguments:
- node_index: int32 [3, 16384], P(None, 'blk'), may hold values from 0 to 63
- emitters: int32 [64], replicated, may hold values from 0 to 16383
- admittance: float32 [2, 16384], P(None, 'blk'), may hold values from -3 to 3
- wavenumbers: float32 [4], P('freq'), may hold values from 20 to 60
Outputs:
- scattered: bfloat16 [4, 2, 64, 16384], P('freq', None, None, 'blk')
- gradient: float32 [16384], P('blk')
All inputs are finite; a program needn't handle non-finite values.
Results may differ from a plain program's by a relative error of at most 0.006.
Values may be sent and summed in bfloat16 or wider, within the bound.
No kernel may reach another device: no remote copies, remote signals or barrier semaphores. Data moves between devices by JAX's collectives and lax.ppermute only.
A program may use at most 64 MiB of HBM per device.

v0:
```python
import jax
import jax.numpy as jnp
from jax import lax
from jax.sharding import Mesh
from jax.sharding import PartitionSpec as P

GRID = 64
BLK = ("blk_0", "blk_1", "blk_2")
soften = 0.0025


def in_order(blocks, dim):
    blocks = jnp.moveaxis(blocks, 0, dim)
    shape = blocks.shape
    return blocks.reshape(*shape[:dim], shape[dim] * shape[dim + 1], *shape[dim + 2 :])


def all_blocks(value, axes, turns):
    blocks = value
    for k in turns:
        blocks = lax.all_gather(blocks, axes[k])
    done = turns[::-1]
    back = [done.index(k) for k in range(len(axes))]
    blocks = blocks.transpose(*back, *range(len(axes), blocks.ndim))
    return blocks.reshape(-1, *value.shape)


def gather_axes(value, axes, turns, dim):
    return in_order(all_blocks(value, axes, turns), dim)


def copy_for_each(value, axis):
    copies = jnp.broadcast_to(value, (lax.axis_size(axis), *value.shape))
    return lax.all_to_all(copies, axis, split_axis=0, concat_axis=0, tiled=True)


def taken_together(value, axis):
    return copy_for_each(value, axis).sum(axis=0)


def green_tile(row_places, col_places, wavenum, strength):
    separation = row_places[:, :, None] - col_places[:, None, :]
    radius = jnp.sqrt(jnp.sum(separation * separation, axis=0) + soften)
    amplitude = strength / radius
    phase_turn = wavenum * radius
    return jnp.stack([amplitude * jnp.cos(phase_turn), amplitude * jnp.sin(phase_turn)]).astype(
        jnp.bfloat16
    )


def apply_tile(tile_data, source):
    real_part = jnp.einsum(
        "tc,rc->tr", source[0], tile_data[0], preferred_element_type=jnp.float32
    ) - jnp.einsum("tc,rc->tr", source[1], tile_data[1], preferred_element_type=jnp.float32)
    imag_part = jnp.einsum(
        "tc,rc->tr", source[1], tile_data[0], preferred_element_type=jnp.float32
    ) + jnp.einsum("tc,rc->tr", source[0], tile_data[1], preferred_element_type=jnp.float32)
    return jnp.stack([real_part, imag_part])


def complex_scale(factor_pair, field_pair):
    factor_real = factor_pair[0][None, :]
    factor_imag = factor_pair[1][None, :]
    real_part = factor_real * field_pair[0] - factor_imag * field_pair[1]
    imag_part = factor_real * field_pair[1] + factor_imag * field_pair[0]
    return jnp.stack([real_part, imag_part])


def row_potential(places, own_places, wavenum, strength, block_count, row_count):
    group_blocks = 1
    for candidate in range(1, block_count + 1):
        if block_count % candidate == 0 and candidate * row_count <= 4096:
            group_blocks = candidate
    group_cols = group_blocks * row_count

    def make_tile(group_id):
        col_places = lax.dynamic_slice_in_dim(places, group_id * group_cols, group_cols, 1)
        return green_tile(own_places, col_places, wavenum, strength)

    tile_stack = lax.map(make_tile, jnp.arange(block_count // group_blocks, dtype=jnp.int32))
    tile_flat = jnp.transpose(tile_stack, (1, 2, 0, 3)).reshape(
        2, row_count, block_count * row_count
    )

    def potential(source, whole_source):
        if whole_source is None:
            whole_source = gather_axes(source, BLK, (0, 1, 2), 2)
        return apply_tile(tile_flat, whole_source)

    return potential


def local(node_index, emitters, admittance, wavenumbers):
    block_count = lax.axis_size(BLK)
    lane_count = lax.axis_size("freq")
    row_count = node_index.shape[1]
    node_count = block_count * row_count
    emitter_count = emitters.shape[0]
    own_block = lax.axis_index(BLK)
    every_index = lax.all_gather(node_index, BLK, axis=1, tiled=True)
    places = every_index.astype(jnp.float32) / GRID
    own_places = node_index.astype(jnp.float32) / GRID
    wavenum = wavenumbers[0]
    strength = float(node_count) ** (-0.5)
    emitter_places = places[:, emitters]
    incident_whole = green_tile(emitter_places, places, wavenum, 1.0)
    incident = lax.dynamic_slice_in_dim(incident_whole, own_block * row_count, row_count, 2)
    potential = row_potential(places, own_places, wavenum, strength, block_count, row_count)
    first_wave = potential(incident, incident_whole)
    weighted = complex_scale(admittance, first_wave).astype(jnp.bfloat16)
    second = potential(weighted, None)
    lane_terms = jnp.sum(first_wave[0] * second[0] - first_wave[1] * second[1], axis=0) / (
        lane_count * emitter_count
    )
    gradient = taken_together(lane_terms, "freq")
    return (second.astype(jnp.bfloat16)[None], gradient)


def solution(mesh):
    split = Mesh(
        mesh.devices.reshape(4, 8, 4, mesh.shape["freq"]), ("blk_0", "blk_1", "blk_2", "freq")
    )
    in_specs = (P(None, BLK), P(), P(None, BLK), P("freq"))
    out_specs = (P("freq", None, None, BLK), P(BLK))
    return jax.shard_map(local, mesh=split, in_specs=in_specs, out_specs=out_specs, check_vma=False)
```

profile of v0, /device:TPU:1, one launch (start us, length us, event | category | flops | bytes accessed | tf_op | source)
XLA Modules:
  0.0 678.0 jit_solution(9046614232390934011)
XLA Ops:
  7.2 0.8 copy.41
  8.7 366.5 %all_gather.19 = s32[3,16384]{0,1:T(8,128)S(1)} all-gather(s32[3,128]{0,1:T(8,128)S(1)} %copy.41), channel_id=1, replica_groups=mesh['blk_0'=4,'blk_1'=8,'blk_2'=4,'freq'=4] {'blk_0','blk_1','blk_2'}, dimensions={1}, use_global_device_ids=true | all-gather | bytes 198144 | tf_op jit(solution)/shard_map/all_gather | solution.py:100
  375.2 3.5 convert_multiply_fusion
  378.8 5.5 copy.43
  384.3 4.0 gather_fusion
  389.0 3.6 multiply_reduce_fusion.1
  392.5 68.6 %while.10 = (s32[]{:T(128)}, bf16[4,2,128,4096]{2,3,0,1:T(8,128)(2,1)}, f32[3,128]{1,0:T(4,128)S(1)}, s32[4]{0:T(128)S(1)}, f32[3,16384]{1,0:T(4,128)S(1)}, /*in...) while((s32[]{:T(128)}, bf16[4,2,128,4096]{2,3,0,1:T(8,128)(2,1)}, f32[3,128]{1,0:T(4,128)S(1)}, ...), condition=%wide.region_3.4_spmd, body=%wide.region_1.3_spmd.sunk | while | flops 8912902 | bytes 19023540 | solution.py:80
  393.8 0.9 multiply_reduce_fusion.3
  394.6 8.9 %fusion.43 = (bf16[1,1,128,4096]{3,2,1,0:T(8,128)(2,1)S(1)}, bf16[1,1,128,4096]{3,2,1,0:T(8,128)(2,1)S(1)}) fusion(f32[]{:T(128)} %get-tuple-element.164, f32[128,4096]{1,0:T(8,128)S(1)} %multiply_reduce_fusion.3), kind=kLoop, calls=%fused_computation.7.clone.1 | loop fusion | flops 3670016 | bytes 4194308 | tf_op jit(solution)/shard_map/while/body/eval_jaxpr/stack | solution.py:46
  403.6 1.5 pad_maximum_fusion.4
  405.1 3.1 copy.77
  408.2 1.4 constant_dynamic-update-slice_fusion.2
  410.9 0.9 multiply_reduce_fusion.3
  411.8 8.9 %fusion.43 = (bf16[1,1,128,4096]{3,2,1,0:T(8,128)(2,1)S(1)}, bf16[1,1,128,4096]{3,2,1,0:T(8,128)(2,1)S(1)}) fusion(f32[]{:T(128)} %get-tuple-element.164, f32[128,4096]{1,0:T(8,128)S(1)} %multiply_reduce_fusion.3), kind=kLoop, calls=%fused_computation.7.clone.1 | loop fusion | flops 3670016 | bytes 4194308 | tf_op jit(solution)/shard_map/while/body/eval_jaxpr/stack | solution.py:46
  420.7 1.5 pad_maximum_fusion.4
  422.2 3.1 copy.77
  425.4 1.5 constant_dynamic-update-slice_fusion.2
  428.1 0.9 multiply_reduce_fusion.3
  428.9 8.9 %fusion.43 = (bf16[1,1,128,4096]{3,2,1,0:T(8,128)(2,1)S(1)}, bf16[1,1,128,4096]{3,2,1,0:T(8,128)(2,1)S(1)}) fusion(f32[]{:T(128)} %get-tuple-element.164, f32[128,4096]{1,0:T(8,128)S(1)} %multiply_reduce_fusion.3), kind=kLoop, calls=%fused_computation.7.clone.1 | loop fusion | flops 3670016 | bytes 4194308 | tf_op jit(solution)/shard_map/while/body/eval_jaxpr/stack | solution.py:46
  437.9 1.5 pad_maximum_fusion.4
  439.4 3.1 copy.77
  442.5 1.5 constant_dynamic-update-slice_fusion.2
  445.2 0.9 multiply_reduce_fusion.3
  446.1 8.9 %fusion.43 = (bf16[1,1,128,4096]{3,2,1,0:T(8,128)(2,1)S(1)}, bf16[1,1,128,4096]{3,2,1,0:T(8,128)(2,1)S(1)}) fusion(f32[]{:T(128)} %get-tuple-element.164, f32[128,4096]{1,0:T(8,128)S(1)} %multiply_reduce_fusion.3), kind=kLoop, calls=%fused_computation.7.clone.1 | loop fusion | flops 3670016 | bytes 4194308 | tf_op jit(solution)/shard_map/while/body/eval_jaxpr/stack | solution.py:46
  455.0 1.5 pad_maximum_fusion.4
  456.6 3.1 copy.77
  459.7 1.5 constant_dynamic-update-slice_fusion.2
  461.2 3.9 fusion.24
  465.1 0.7 copy-done.4
  465.8 16.6 %multiply_convert_fusion.2 = (bf16[64,16384]{1,0:T(8,128)(2,1)S(1)}, bf16[64,16384]{1,0:T(8,128)(2,1)S(1)}) fusion(f32[64,16384]{1,0:T(8,128)S(1)} %copy-done.4, f32[]{:T(128)} %bitcast.66), kind=kLoop, calls=%fused_computation.13 | loop fusion | flops 7340032 | bytes 8388612 | tf_op jit(solution)/shard_map/slice | solution.py:54
  482.5 0.9 fusion.29
  483.3 0.9 fusion.28
  484.2 0.9 convolution_add_fusion
  485.1 0.9 convolution_subtract_fusion
  486.0 11.2 %all_gather.20 = bf16[4,2,64,128]{3,2,1,0:T(8,128)(2,1)} all-gather(bf16[1,2,64,128]{3,2,1,0:T(8,128)(2,1)S(1)} %pad_maximum_fusion.1), channel_id=1, replica_groups=mesh['blk_0'=4,'blk_1'=8,'blk_2'=4,'freq'=4] {'blk_0'}, dimensions={0}, use_global_device_ids=true | all-gather | bytes 163840 | tf_op jit(solution)/shard_map/all_gather | solution.py:21
  497.4 84.1 %all-gather.5.cloned.1.call-done = bf16[32,2,64,128]{3,2,1,0:T(8,128)(2,1)} async-done(((bf16[4,2,64,128]{3,2,1,0:T(8,128)(2,1)}), bf16[32,2,64,128]{3,2,1,0:T(8,128)(2,1)}) %all-gather.5.cloned.1.call-update) | async-done | bytes 1048592 | tf_op jit(solution)/shard_map/all_gather | solution.py:21
  581.6 59.3 %all-gather.7.cloned.1.call-done = bf16[32,4,2,64,128]{4,3,2,1,0:T(8,128)(2,1)} async-done(((bf16[8,4,2,64,128]{4,3,2,1,0:T(8,128)(2,1)}), bf16[32,4,2,64,128]{4,3,2,1,0:T(8,128)(2,1)}) %all-gather.7.cloned.1.call-update) | async-done | bytes 4194320 | tf_op jit(solution)/shard_map/all_gather | solution.py:21
  640.8 3.1 copy.46
  644.0 1.0 fusion.25
  645.0 1.4 copy.48
  646.3 0.8 copy-done.1
  647.2 1.6 fusion.6
  648.8 1.6 fusion.4
  650.4 1.4 copy.47
  651.7 1.6 fusion.16
  653.3 1.5 subtract_reduce_fusion
  655.5 8.2 %all-to-all-start = ((f32[4,1,128]{2,1,0:T(1,128)}), f32[4,1,128]{2,1,0:T(1,128)S(1)}, u32[]{:S(2)}, u32[]{:S(2)}) async-start(f32[4,1,128]{2,1,0:T(1,128)} %broadcast_in_dim.18), calls=%async_computation | async-start | bytes 4096 | tf_op jit(solution)/shard_map/all_to_all | solution.py:34
  664.3 6.4 all-to-all-done
  (37 shorter events, 5.3 us)
Async XLA Ops:
  7.2 574.4 %all-gather.5.cloned.1.call-start = ((), (), s32[]{:S(2)}) async-start(), calls=%async_computation.1 | async-start | bytes 1179648 | tf_op jit(solution)/shard_map/all_gather | solution.py:21
  378.8 5.5 copy-start.6
  461.2 4.7 copy-start.4
  465.1 18.2 %copy-start.2 = (bf16[1,128,4,4096]{1,3,2,0:T(8,128)(2,1)}, bf16[1,128,4,4096]{1,3,2,0:T(8,128)(2,1)S(1)}, u32[]{:S(2)}) copy-start(bf16[1,128,4,4096]{1,3,2,0:T(8,128)(2,1)S(1)} %get-tuple-element.86) | copy-start | bytes 12582916
  465.1 20.0 %copy-start = (bf16[1,128,4,4096]{1,3,2,0:T(8,128)(2,1)}, bf16[1,128,4,4096]{1,3,2,0:T(8,128)(2,1)S(1)}, u32[]{:S(2)}) copy-start(bf16[1,128,4,4096]{1,3,2,0:T(8,128)(2,1)S(1)} %get-tuple-element.85) | copy-start | bytes 12582916
  485.1 0.9 copy-start.5
  497.2 143.6 %all-gather.7.cloned.1.call-start = ((), (), s32[]{:S(2)}) async-start(), calls=%async_computation.2 | async-start | bytes 5242880 | tf_op jit(solution)/shard_map/all_gather | solution.py:21
  645.0 2.2 copy-start.1
  646.3 2.4 copy-start.3
  655.5 15.2 %all-to-all-start = ((f32[4,1,128]{2,1,0:T(1,128)}), f32[4,1,128]{2,1,0:T(1,128)S(1)}, u32[]{:S(2)}, u32[]{:S(2)}) async-start(f32[4,1,128]{2,1,0:T(1,128)} %broadcast_in_dim.18), calls=%async_computation | async-start | bytes 4096 | tf_op jit(solution)/shard_map/all_to_all | solution.py:34
Sparse Core Ops, SparseCore 0:
  497.3 84.1 all-gather.4
  583.6 57.1 all-gather.6
where the time goes:
time: 679 us; the launch traced here: 678 us
  blocking collectives  378 us (56%)
  waiting for transfers between devices  150 us (22%)
  other arithmetic  70.8 us (10%)
  local copies, waits for them, and re-layouts  43.9 us (6%)
  between operations  14.9 us (2%)
  matrix products  9.75 us (1%)
  starting transfers between devices  8.47 us (1%)
    all_gather x1, blocking collectives, local(): every_index = lax.all_gather(node_index, BLK, axis=1, tiled=True)  367 us
    all_gather x2, waiting for transfers between devices, all_blocks(): blocks = lax.all_gather(blocks, axes[k])  143 us
    another operation x8, other arithmetic, green_tile(): jnp.stack([amplitude * jnp.cos(phase_turn), amplitude * jnp.sin(phase_tur...  41.8 us
    dynamic_update_slice x8, local copies, waits for them, and re-layouts, row_potential(): lax.map(make_tile, jnp.arange(block_count // group_blocks, dtype=jnp.int32))  18.3 us
    slice x1, other arithmetic, apply_tile(): source[1]  16.6 us
  transfers between devices with their start and end apart: 3, of which 3 were waited for; matrix products, arithmetic and copies ran while one was open for 0% of the time, Pallas kernels for 0%

commit v1 on v0

--- a/solution.py
+++ b/solution.py
@@ -97,7 +97,10 @@
     node_count = block_count * row_count
     emitter_count = emitters.shape[0]
     own_block = lax.axis_index(BLK)
-    every_index = lax.all_gather(node_index, BLK, axis=1, tiled=True)
+    count = lax.axis_size(BLK)
+    pieces = jnp.stack([node_index for _ in range(count)])
+    pieces = lax.all_to_all(pieces, BLK, split_axis=0, concat_axis=0)
+    every_index = jnp.concatenate(pieces, axis=1)
     places = every_index.astype(jnp.float32) / GRID
     own_places = node_index.astype(jnp.float32) / GRID
     wavenum = wavenumbers[0]

time: 679 us -> 296 us (0.44)
  blocking collectives: 378 us -> 11.6 us
  waiting for transfers between devices: 150 us -> 112 us
  starting transfers between devices: 8.47 us -> 26.2 us
    all_gather x1 -> x0, blocking collectives: 367 us -> none  [local(): every_index = lax.all_gather(node_index, BLK, axis=1, tiled=True)]
    all_gather x2, waiting for transfers between devices: 143 us -> 95.7 us  [all_blocks(): blocks = lax.all_gather(blocks, axes[k])]
    all_to_all x0 -> x1, starting transfers between devices: none -> 17.8 us  [local(): pieces = lax.all_to_all(pieces, BLK, split_axis=0, concat_axis=0)]
    all_to_all x0 -> x1, waiting for transfers between devices: none -> 10.2 us  [local(): pieces = lax.all_to_all(pieces, BLK, split_axis=0, concat_axis=0)]
  transfers between devices with their start and end apart: 3 -> 4, of which waited for: 3 -> 4; matrix products, arithmetic and copies ran while one was open for 0% -> 1% of each run, Pallas kernels for 0% -> 0%
where the time goes in v1:
time: 296 us
  waiting for transfers between devices  112 us (38%)
  other arithmetic  68 us (23%)
  local copies, waits for them, and re-layouts  50.2 us (17%)
  starting transfers between devices  26.2 us (9%)
  between operations  14.9 us (5%)
  blocking collectives  11.6 us (4%)
  matrix products  9.74 us (3%)
    all_gather x2, waiting for transfers between devices, all_blocks(): blocks = lax.all_gather(blocks, axes[k])  95.7 us
    another operation x8, other arithmetic, green_tile(): jnp.stack([amplitude * jnp.cos(phase_turn), amplitude * jnp.sin(phase_tur...  41.8 us
    dynamic_update_slice x8, local copies, waits for them, and re-layouts, row_potential(): lax.map(make_tile, jnp.arange(block_count // group_blocks, dtype=jnp.int32))  18.3 us
    all_to_all x1, starting transfers between devices, local(): pieces = lax.all_to_all(pieces, BLK, split_axis=0, concat_axis=0)  17.8 us
    slice x1, other arithmetic, apply_tile(): source[1]  16.6 us
    all_gather x1, blocking collectives, all_blocks(): blocks = lax.all_gather(blocks, axes[k])  11.6 us
    div x2, local copies, waits for them, and re-layouts, local(): places = every_index.astype(jnp.float32) / GRID  10.3 us
    all_to_all x1, waiting for transfers between devices, local(): pieces = lax.all_to_all(pieces, BLK, split_axis=0, concat_axis=0)  10.2 us
  transfers between devices with their start and end apart: 4, of which 4 were waited for; matrix products, arithmetic and copies ran while one was open for 1% of the time, Pallas kernels for 0%

profile of v1, /device:TPU:1, one launch (start us, length us, event | category | flops | bytes accessed | tf_op | source)
XLA Modules:
  0.0 295.6 jit_solution(10298264470148744374)
XLA Ops:
  7.2 1.4 stack.21
  8.6 17.8 %all-to-all-start = ((s32[128,3,128]{2,1,0:T(4,128)}), s32[128,3,128]{2,1,0:T(4,128)S(1)}, u32[]{:S(2)}, u32[]{:S(2)}) async-start(s32[128,3,128]{2,1,0:T(4,128)} %stack.21), calls=%async_computation | async-start | bytes 524288 | tf_op jit(solution)/shard_map/all_to_all | solution.py:102
  29.2 10.2 %all-to-all-done = s32[128,3,128]{2,1,0:T(4,128)S(1)} async-done(((s32[128,3,128]{2,1,0:T(4,128)}), s32[128,3,128]{2,1,0:T(4,128)S(1)}, u32[]{:S(2)}, u32[]{:S(2)}) %all-to-all-start) | async-done | bytes 196640 | tf_op jit(solution)/shard_map/all_to_all | solution.py:102
  39.5 4.9 %copy.41 = f32[3,128,128]{0,2,1:T(8,128)} copy(f32[3,128,128]{2,0,1:T(4,128)S(1)} %multiply_bitcast_fusion) | data formatting | bytes 393216 | tf_op jit(solution)/shard_map/div | solution.py:104
  44.4 5.4 %copy.43 = f32[3,16384]{1,0:T(4,128)S(1)} copy(f32[3,16384]{0,1:T(8,128)} %bitcast.78) | data formatting | bytes 393216 | tf_op jit(solution)/shard_map/div | solution.py:104
  49.8 4.0 %gather_fusion = f32[64,3]{1,0:T(8,128)S(1)} fusion(f32[3,16384]{0,1:T(8,128)} %bitcast.79, s32[1024]{0:T(1024)S(1)} %pad_clamp_fusion), kind=kCustom, calls=%fused_computation | custom fusion | bytes 1792 | tf_op jit(solution)/shard_map/gather | solution.py:108
  53.9 3.6 %multiply_reduce_fusion.1 = f32[64,16384]{1,0:T(8,128)} fusion(f32[3,16384]{1,0:T(4,128)S(1)} %copy.43, f32[3,64]{1,0:T(4,128)S(1)} %copy.42), kind=kLoop, calls=%fused_computation.11 | loop fusion | flops 8388608 | bytes 4391680 | tf_op jit(solution)/shard_map/reduce_sum | solution.py:43
  57.5 68.6 %while.10 = (s32[]{:T(128)}, bf16[4,2,128,4096]{2,3,0,1:T(8,128)(2,1)}, f32[3,128]{1,0:T(4,128)S(1)}, s32[4]{0:T(128)S(1)}, f32[3,16384]{1,0:T(4,128)S(1)}, /*in...) while((s32[]{:T(128)}, bf16[4,2,128,4096]{2,3,0,1:T(8,128)(2,1)}, f32[3,128]{1,0:T(4,128)S(1)}, ...), condition=%wide.region_3.4_spmd, body=%wide.region_1.3_spmd.sunk | while | flops 8912902 | bytes 19023540 | solution.py:80
  58.7 0.9 multiply_reduce_fusion.3
  59.6 8.9 %fusion.43 = (bf16[1,1,128,4096]{3,2,1,0:T(8,128)(2,1)S(1)}, bf16[1,1,128,4096]{3,2,1,0:T(8,128)(2,1)S(1)}) fusion(f32[]{:T(128)} %get-tuple-element.164, f32[128,4096]{1,0:T(8,128)S(1)} %multiply_reduce_fusion.3), kind=kLoop, calls=%fused_computation.7.clone.1 | loop fusion | flops 3670016 | bytes 4194308 | tf_op jit(solution)/shard_map/while/body/eval_jaxpr/stack | solution.py:46
  68.5 1.5 pad_maximum_fusion.4
  70.0 3.1 %copy.77 = bf16[1,2,128,4096]{2,3,0,1:T(8,128)(2,1)S(1)} copy(bf16[1,2,128,4096]{3,2,1,0:T(8,128)(2,1)} %pad_maximum_fusion.4) | data formatting | bytes 4194304 | tf_op jit(solution)/shard_map/while/body/jit(dynamic_update_index_in_dim)/dynamic_update_slice | solution.py:80
  73.2 1.4 constant_dynamic-update-slice_fusion.2
  75.8 0.9 multiply_reduce_fusion.3
  76.7 8.9 %fusion.43 = (bf16[1,1,128,4096]{3,2,1,0:T(8,128)(2,1)S(1)}, bf16[1,1,128,4096]{3,2,1,0:T(8,128)(2,1)S(1)}) fusion(f32[]{:T(128)} %get-tuple-element.164, f32[128,4096]{1,0:T(8,128)S(1)} %multiply_reduce_fusion.3), kind=kLoop, calls=%fused_computation.7.clone.1 | loop fusion | flops 3670016 | bytes 4194308 | tf_op jit(solution)/shard_map/while/body/eval_jaxpr/stack | solution.py:46
  85.7 1.5 pad_maximum_fusion.4
  87.2 3.1 %copy.77 = bf16[1,2,128,4096]{2,3,0,1:T(8,128)(2,1)S(1)} copy(bf16[1,2,128,4096]{3,2,1,0:T(8,128)(2,1)} %pad_maximum_fusion.4) | data formatting | bytes 4194304 | tf_op jit(solution)/shard_map/while/body/jit(dynamic_update_index_in_dim)/dynamic_update_slice | solution.py:80
  90.3 1.5 constant_dynamic-update-slice_fusion.2
  93.0 0.9 multiply_reduce_fusion.3
  93.9 8.9 %fusion.43 = (bf16[1,1,128,4096]{3,2,1,0:T(8,128)(2,1)S(1)}, bf16[1,1,128,4096]{3,2,1,0:T(8,128)(2,1)S(1)}) fusion(f32[]{:T(128)} %get-tuple-element.164, f32[128,4096]{1,0:T(8,128)S(1)} %multiply_reduce_fusion.3), kind=kLoop, calls=%fused_computation.7.clone.1 | loop fusion | flops 3670016 | bytes 4194308 | tf_op jit(solution)/shard_map/while/body/eval_jaxpr/stack | solution.py:46
  102.8 1.5 pad_maximum_fusion.4
  104.3 3.1 %copy.77 = bf16[1,2,128,4096]{2,3,0,1:T(8,128)(2,1)S(1)} copy(bf16[1,2,128,4096]{3,2,1,0:T(8,128)(2,1)} %pad_maximum_fusion.4) | data formatting | bytes 4194304 | tf_op jit(solution)/shard_map/while/body/jit(dynamic_update_index_in_dim)/dynamic_update_slice | solution.py:80
  107.5 1.5 constant_dynamic-update-slice_fusion.2
  110.2 0.9 multiply_reduce_fusion.3
  111.0 8.9 %fusion.43 = (bf16[1,1,128,4096]{3,2,1,0:T(8,128)(2,1)S(1)}, bf16[1,1,128,4096]{3,2,1,0:T(8,128)(2,1)S(1)}) fusion(f32[]{:T(128)} %get-tuple-element.164, f32[128,4096]{1,0:T(8,128)S(1)} %multiply_reduce_fusion.3), kind=kLoop, calls=%fused_computation.7.clone.1 | loop fusion | flops 3670016 | bytes 4194308 | tf_op jit(solution)/shard_map/while/body/eval_jaxpr/stack | solution.py:46
  120.0 1.5 pad_maximum_fusion.4
  121.5 3.1 %copy.77 = bf16[1,2,128,4096]{2,3,0,1:T(8,128)(2,1)S(1)} copy(bf16[1,2,128,4096]{3,2,1,0:T(8,128)(2,1)} %pad_maximum_fusion.4) | data formatting | bytes 4194304 | tf_op jit(solution)/shard_map/while/body/jit(dynamic_update_index_in_dim)/dynamic_update_slice | solution.py:80
  124.6 1.5 constant_dynamic-update-slice_fusion.2
  126.1 3.9 %fusion.24 = (bf16[1,128,4,4096]{1,3,2,0:T(8,128)(2,1)S(1)}, bf16[1,128,4,4096]{1,3,2,0:T(8,128)(2,1)S(1)}) fusion(bf16[2,128,4,4096]{1,3,2,0:T(8,128)(2,1)} %bitcast.85), kind=kLoop, calls=%fused_computation.48 | loop fusion | bytes 16777216 | tf_op jit(solution)/shard_map/slice | solution.py:54
  130.7 16.6 %multiply_convert_fusion.2 = (bf16[64,16384]{1,0:T(8,128)(2,1)S(1)}, bf16[64,16384]{1,0:T(8,128)(2,1)S(1)}) fusion(f32[64,16384]{1,0:T(8,128)S(1)} %copy-done.4, f32[]{:T(128)} %bitcast.69), kind=kLoop, calls=%fused_computation.12 | loop fusion | flops 7340032 | bytes 8388612 | tf_op jit(solution)/shard_map/slice | solution.py:54
  147.4 0.9 fusion.29
  148.3 0.9 fusion.28
  149.1 0.9 convolution_add_fusion
  150.0 0.9 convolution_subtract_fusion
  150.9 11.6 %all_gather.16 = bf16[4,2,64,128]{3,2,1,0:T(8,128)(2,1)} all-gather(bf16[1,2,64,128]{3,2,1,0:T(8,128)(2,1)S(1)} %pad_maximum_fusion.1), channel_id=1, replica_groups=mesh['blk_0'=4,'blk_1'=8,'blk_2'=4,'freq'=4] {'blk_0'}, dimensions={0}, use_global_device_ids=true | all-gather | bytes 163840 | tf_op jit(solution)/shard_map/all_gather | solution.py:21
  162.7 36.4 %all-gather.5.cloned.1.call-done = bf16[32,2,64,128]{3,2,1,0:T(8,128)(2,1)} async-done(((bf16[4,2,64,128]{3,2,1,0:T(8,128)(2,1)}), bf16[32,2,64,128]{3,2,1,0:T(8,128)(2,1)}) %all-gather.5.cloned.1.call-update) | async-done | bytes 1048592 | tf_op jit(solution)/shard_map/all_gather | solution.py:21
  199.2 59.3 %all-gather.7.cloned.1.call-done = bf16[32,4,2,64,128]{4,3,2,1,0:T(8,128)(2,1)} async-done(((bf16[8,4,2,64,128]{4,3,2,1,0:T(8,128)(2,1)}), bf16[32,4,2,64,128]{4,3,2,1,0:T(8,128)(2,1)}) %all-gather.7.cloned.1.call-update) | async-done | bytes 4194320 | tf_op jit(solution)/shard_map/all_gather | solution.py:21
  258.4 3.1 %copy.46 = bf16[4,8,4,2,64,128]{5,4,3,2,1,0:T(8,128)(2,1)S(1)} copy(bf16[4,8,4,2,64,128]{5,4,3,0,1,2:T(8,128)(2,1)} %bitcast.86) | data formatting | bytes 8388608 | tf_op jit(solution)/shard_map/transpose | solution.py:24
  261.6 1.0 fusion.25
  262.6 1.4 copy.48
  263.9 0.8 copy-done.1
  264.8 1.6 fusion.6
  266.4 1.6 fusion.4
  268.0 1.4 copy.47
  269.3 1.6 fusion.16
  270.9 1.5 subtract_reduce_fusion
  273.1 8.2 %all-to-all-start.1 = ((f32[4,1,128]{2,1,0:T(1,128)}), f32[4,1,128]{2,1,0:T(1,128)S(1)}, u32[]{:S(2)}, u32[]{:S(2)}) async-start(f32[4,1,128]{2,1,0:T(1,128)} %broadcast_in_dim.18), calls=%async_computation.1 | async-start | bytes 4096 | tf_op jit(solution)/shard_map/all_to_all | solution.py:34
  281.9 6.4 %all-to-all-done.1 = f32[4,1,128]{2,1,0:T(1,128)S(1)} async-done(((f32[4,1,128]{2,1,0:T(1,128)}), f32[4,1,128]{2,1,0:T(1,128)S(1)}, u32[]{:S(2)}, u32[]{:S(2)}) %all-to-all-start.1) | async-done | bytes 2080 | tf_op jit(solution)/shard_map/all_to_all | solution.py:34
  (35 shorter events, 7.5 us)
Async XLA Ops:
  8.6 30.8 %all-to-all-start = ((s32[128,3,128]{2,1,0:T(4,128)}), s32[128,3,128]{2,1,0:T(4,128)S(1)}, u32[]{:S(2)}, u32[]{:S(2)}) async-start(s32[128,3,128]{2,1,0:T(4,128)} %stack.21), calls=%async_computation | async-start | bytes 524288 | tf_op jit(solution)/shard_map/all_to_all | solution.py:102
  26.4 172.8 %all-gather.5.cloned.1.call-start = ((), (), s32[]{:S(2)}) async-start(), calls=%async_computation.2 | async-start | bytes 1179648 | tf_op jit(solution)/shard_map/all_gather | solution.py:21
  126.1 4.7 %copy-start.4 = (f32[64,16384]{1,0:T(8,128)S(1)}, f32[64,16384]{1,0:T(8,128)}, u32[]{:S(2)}) copy-start(f32[64,16384]{1,0:T(8,128)} %multiply_reduce_fusion.1) | copy-start | bytes 12582916
  130.0 18.2 %copy-start.2 = (bf16[1,128,4,4096]{1,3,2,0:T(8,128)(2,1)}, bf16[1,128,4,4096]{1,3,2,0:T(8,128)(2,1)S(1)}, u32[]{:S(2)}) copy-start(bf16[1,128,4,4096]{1,3,2,0:T(8,128)(2,1)S(1)} %get-tuple-element.86) | copy-start | bytes 12582916
  130.0 20.0 %copy-start = (bf16[1,128,4,4096]{1,3,2,0:T(8,128)(2,1)}, bf16[1,128,4,4096]{1,3,2,0:T(8,128)(2,1)S(1)}, u32[]{:S(2)}) copy-start(bf16[1,128,4,4096]{1,3,2,0:T(8,128)(2,1)S(1)} %get-tuple-element.85) | copy-start | bytes 12582916
  162.5 95.9 %all-gather.7.cloned.1.call-start = ((), (), s32[]{:S(2)}) async-start(), calls=%async_computation.3 | async-start | bytes 5242880 | tf_op jit(solution)/shard_map/all_gather | solution.py:21
  262.6 2.2 copy-start.1
  263.9 2.4 copy-start.3
  273.1 15.2 %all-to-all-start.1 = ((f32[4,1,128]{2,1,0:T(1,128)}), f32[4,1,128]{2,1,0:T(1,128)S(1)}, u32[]{:S(2)}, u32[]{:S(2)}) async-start(f32[4,1,128]{2,1,0:T(1,128)} %broadcast_in_dim.18), calls=%async_computation.1 | async-start | bytes 4096 | tf_op jit(solution)/shard_map/all_to_all | solution.py:34
Sparse Core Ops, SparseCore 0:
  162.6 36.4 all-gather.4
  201.2 57.1 all-gather.6
